TPU v7x, 8 devices: a whole 2x2x1 slice. The times are simulated.
8 devices in a mesh: row: 2 (over z, y), col: 4 (over x, core).
Axes of the slice: x: 2, y: 2, z: 1, core: 2. Of those that a mesh axis runs over, the one named last changes fastest.
Arguments:
- v_panels: float32 [8192, 8192], P('row', 'col')
- t_factors: float32 [128, 64, 64], P('col')
- z_vecs: float32 [8192, 2048], P(None, ('row', 'col'))
Outputs:
- output: float32 [8192, 2048], P(None, ('row', 'col'))
All inputs are finite; a program needn't handle non-finite values.
Results may differ from a plain program's by a relative error of at most 0.001.
Values sent between devices are 32-bit elements.
A program may use at most 1 GiB of HBM per device.

v0:
```python
import jax
import jax.numpy as jnp
from jax import lax
from jax.sharding import PartitionSpec as P, NamedSharding

FULL_PREC = lax.Precision.HIGHEST
CONTRACT_ROWS = (((0,), (0,)), ((), ()))


def solution(mesh):
    col_dev = mesh.shape["col"]

    def local_apply(v_loc, t_loc, z_loc):
        num_local = t_loc.shape[0]
        block_w = t_loc.shape[1]
        x_two = lax.all_to_all(z_loc, "row", 0, 1, tiled=True)

        def outer_step(step_idx, x_cur):
            local_idx = num_local - 1 - step_idx
            v_own = lax.dynamic_slice_in_dim(v_loc, local_idx * block_w, block_w, axis=1)
            t_own = lax.dynamic_index_in_dim(t_loc, local_idx, axis=0, keepdims=False)
            v_all = lax.all_gather(v_own, "col")
            t_all = lax.all_gather(t_own, "col")

            def inner_step(sub_idx, x_in):
                owner_col = col_dev - 1 - sub_idx
                v_blk = v_all[owner_col]
                t_blk = t_all[owner_col]
                w_part = lax.dot_general(v_blk, x_in, CONTRACT_ROWS, precision=FULL_PREC, preferred_element_type=jnp.float32)
                w_sum = lax.psum(w_part, "row")
                y_blk = jnp.dot(t_blk, w_sum, precision=FULL_PREC, preferred_element_type=jnp.float32)
                return x_in - jnp.dot(v_blk, y_blk, precision=FULL_PREC, preferred_element_type=jnp.float32)

            return lax.fori_loop(0, col_dev, inner_step, x_cur)

        x_two = lax.fori_loop(0, num_local, outer_step, x_two)
        return lax.all_to_all(x_two, "row", 1, 0, tiled=True)

    return jax.shard_map(
        local_apply,
        mesh=mesh,
        in_specs=(P("row", "col"), P("col", None, None), P(None, ("row", "col"))),
        out_specs=P(None, ("row", "col")),
        check_vma=False,
    )
```

profile of v0, /device:TPU:0, one launch (start us, length us, event | category | flops | bytes accessed | tf_op | source)
XLA Modules:
  0.0 7007.5 jit_solution(7675331429924130326)
XLA Ops:
  13.5 94.0 %all-to-all-done = f32[2,4096,256]{2,1,0:T(8,128)} async-done(((f32[2,4096,256]{2,1,0:T(8,128)}), f32[2,4096,256]{2,1,0:T(8,128)}, u32[]{:S(2)}, u32[]{:S(2)}) %all-to-all-start) | async-done | bytes 8388640 | tf_op jit(solution)/shard_map/all_to_all | solution.py:16
  125.3 6772.9 %while.44 = (s32[]{:T(128)}, f32[4096,512]{1,0:T(8,128)}, f32[4096,2048]{1,0:T(8,128)}, f32[32,64,64]{2,1,0:T(8,128)}, s32[]{:T(128)}, /*index=5*/s32[]{:T(128)}...) while((s32[]{:T(128)}, f32[4096,512]{1,0:T(8,128)}, ...), condition=%wide.region_4.5_spmd, body=%wide.region_0.4_spmd.sunk | while | flops 3248521216 | bytes 53887512 | solution.py:36
  138.2 46.7 all-gather.5.cloned.1.call-done
  185.0 152.2 %while.45 = (s32[]{:T(128)}, f32[4096,512]{1,0:T(8,128)}, f32[4,4096,64]{2,1,0:T(8,128)}, f32[4,64,64]{2,1,0:T(8,128)S(1)}, s32[]{:T(128)}, /*index=5*/s32[]{:T(128)}, s32[]{:T(128)}, s32[]{:T(128)}) while((s32[]{:T(128)}, f32[4096,512]{1,0:T(8,128)}, f32[4,4096,64]{2,1,0:T(8,128)}, f32[4,64,64]{2,1,0:T(8,128)S(1)}, s32[]{:T(128)}, ...), condition=%wide.region_3.3_spmd, body=%wide.region_1.2_spmd.sunk | while | flops 3248521216 | bytes 30703800 | solution.py:34
  349.9 46.7 all-gather.5.cloned.1.call-done
  396.6 152.2 %while.45 = (s32[]{:T(128)}, f32[4096,512]{1,0:T(8,128)}, f32[4,4096,64]{2,1,0:T(8,128)}, f32[4,64,64]{2,1,0:T(8,128)S(1)}, s32[]{:T(128)}, /*index=5*/s32[]{:T(128)}, s32[]{:T(128)}, s32[]{:T(128)}) while((s32[]{:T(128)}, f32[4096,512]{1,0:T(8,128)}, f32[4,4096,64]{2,1,0:T(8,128)}, f32[4,64,64]{2,1,0:T(8,128)S(1)}, s32[]{:T(128)}, ...), condition=%wide.region_3.3_spmd, body=%wide.region_1.2_spmd.sunk | while | flops 3248521216 | bytes 30703800 | solution.py:34
  561.5 46.7 all-gather.5.cloned.1.call-done
  608.2 152.2 %while.45 = (s32[]{:T(128)}, f32[4096,512]{1,0:T(8,128)}, f32[4,4096,64]{2,1,0:T(8,128)}, f32[4,64,64]{2,1,0:T(8,128)S(1)}, s32[]{:T(128)}, /*index=5*/s32[]{:T(128)}, s32[]{:T(128)}, s32[]{:T(128)}) while((s32[]{:T(128)}, f32[4096,512]{1,0:T(8,128)}, f32[4,4096,64]{2,1,0:T(8,128)}, f32[4,64,64]{2,1,0:T(8,128)S(1)}, s32[]{:T(128)}, ...), condition=%wide.region_3.3_spmd, body=%wide.region_1.2_spmd.sunk | while | flops 3248521216 | bytes 30703800 | solution.py:34
  773.2 46.7 all-gather.5.cloned.1.call-done
  819.9 152.2 %while.45 = (s32[]{:T(128)}, f32[4096,512]{1,0:T(8,128)}, f32[4,4096,64]{2,1,0:T(8,128)}, f32[4,64,64]{2,1,0:T(8,128)S(1)}, s32[]{:T(128)}, /*index=5*/s32[]{:T(128)}, s32[]{:T(128)}, s32[]{:T(128)}) while((s32[]{:T(128)}, f32[4096,512]{1,0:T(8,128)}, f32[4,4096,64]{2,1,0:T(8,128)}, f32[4,64,64]{2,1,0:T(8,128)S(1)}, s32[]{:T(128)}, ...), condition=%wide.region_3.3_spmd, body=%wide.region_1.2_spmd.sunk | while | flops 3248521216 | bytes 30703800 | solution.py:34
  984.8 46.7 all-gather.5.cloned.1.call-done
  1031.5 152.2 %while.45 = (s32[]{:T(128)}, f32[4096,512]{1,0:T(8,128)}, f32[4,4096,64]{2,1,0:T(8,128)}, f32[4,64,64]{2,1,0:T(8,128)S(1)}, s32[]{:T(128)}, /*index=5*/s32[]{:T(128)}, s32[]{:T(128)}, s32[]{:T(128)}) while((s32[]{:T(128)}, f32[4096,512]{1,0:T(8,128)}, f32[4,4096,64]{2,1,0:T(8,128)}, f32[4,64,64]{2,1,0:T(8,128)S(1)}, s32[]{:T(128)}, ...), condition=%wide.region_3.3_spmd, body=%wide.region_1.2_spmd.sunk | while | flops 3248521216 | bytes 30703800 | solution.py:34
  1196.5 46.7 all-gather.5.cloned.1.call-done
  1243.2 152.2 %while.45 = (s32[]{:T(128)}, f32[4096,512]{1,0:T(8,128)}, f32[4,4096,64]{2,1,0:T(8,128)}, f32[4,64,64]{2,1,0:T(8,128)S(1)}, s32[]{:T(128)}, /*index=5*/s32[]{:T(128)}, s32[]{:T(128)}, s32[]{:T(128)}) while((s32[]{:T(128)}, f32[4096,512]{1,0:T(8,128)}, f32[4,4096,64]{2,1,0:T(8,128)}, f32[4,64,64]{2,1,0:T(8,128)S(1)}, s32[]{:T(128)}, ...), condition=%wide.region_3.3_spmd, body=%wide.region_1.2_spmd.sunk | while | flops 3248521216 | bytes 30703800 | solution.py:34
  1408.1 46.7 all-gather.5.cloned.1.call-done
  1454.8 152.2 %while.45 = (s32[]{:T(128)}, f32[4096,512]{1,0:T(8,128)}, f32[4,4096,64]{2,1,0:T(8,128)}, f32[4,64,64]{2,1,0:T(8,128)S(1)}, s32[]{:T(128)}, /*index=5*/s32[]{:T(128)}, s32[]{:T(128)}, s32[]{:T(128)}) while((s32[]{:T(128)}, f32[4096,512]{1,0:T(8,128)}, f32[4,4096,64]{2,1,0:T(8,128)}, f32[4,64,64]{2,1,0:T(8,128)S(1)}, s32[]{:T(128)}, ...), condition=%wide.region_3.3_spmd, body=%wide.region_1.2_spmd.sunk | while | flops 3248521216 | bytes 30703800 | solution.py:34
  1619.8 46.7 all-gather.5.cloned.1.call-done
  1666.5 152.2 %while.45 = (s32[]{:T(128)}, f32[4096,512]{1,0:T(8,128)}, f32[4,4096,64]{2,1,0:T(8,128)}, f32[4,64,64]{2,1,0:T(8,128)S(1)}, s32[]{:T(128)}, /*index=5*/s32[]{:T(128)}, s32[]{:T(128)}, s32[]{:T(128)}) while((s32[]{:T(128)}, f32[4096,512]{1,0:T(8,128)}, f32[4,4096,64]{2,1,0:T(8,128)}, f32[4,64,64]{2,1,0:T(8,128)S(1)}, s32[]{:T(128)}, ...), condition=%wide.region_3.3_spmd, body=%wide.region_1.2_spmd.sunk | while | flops 3248521216 | bytes 30703800 | solution.py:34
  1831.4 46.7 all-gather.5.cloned.1.call-done
  1878.1 152.2 %while.45 = (s32[]{:T(128)}, f32[4096,512]{1,0:T(8,128)}, f32[4,4096,64]{2,1,0:T(8,128)}, f32[4,64,64]{2,1,0:T(8,128)S(1)}, s32[]{:T(128)}, /*index=5*/s32[]{:T(128)}, s32[]{:T(128)}, s32[]{:T(128)}) while((s32[]{:T(128)}, f32[4096,512]{1,0:T(8,128)}, f32[4,4096,64]{2,1,0:T(8,128)}, f32[4,64,64]{2,1,0:T(8,128)S(1)}, s32[]{:T(128)}, ...), condition=%wide.region_3.3_spmd, body=%wide.region_1.2_spmd.sunk | while | flops 3248521216 | bytes 30703800 | solution.py:34
  2043.1 46.7 all-gather.5.cloned.1.call-done
  2089.8 152.2 %while.45 = (s32[]{:T(128)}, f32[4096,512]{1,0:T(8,128)}, f32[4,4096,64]{2,1,0:T(8,128)}, f32[4,64,64]{2,1,0:T(8,128)S(1)}, s32[]{:T(128)}, /*index=5*/s32[]{:T(128)}, s32[]{:T(128)}, s32[]{:T(128)}) while((s32[]{:T(128)}, f32[4096,512]{1,0:T(8,128)}, f32[4,4096,64]{2,1,0:T(8,128)}, f32[4,64,64]{2,1,0:T(8,128)S(1)}, s32[]{:T(128)}, ...), condition=%wide.region_3.3_spmd, body=%wide.region_1.2_spmd.sunk | while | flops 3248521216 | bytes 30703800 | solution.py:34
  2254.7 46.7 all-gather.5.cloned.1.call-done
  2301.4 152.2 %while.45 = (s32[]{:T(128)}, f32[4096,512]{1,0:T(8,128)}, f32[4,4096,64]{2,1,0:T(8,128)}, f32[4,64,64]{2,1,0:T(8,128)S(1)}, s32[]{:T(128)}, /*index=5*/s32[]{:T(128)}, s32[]{:T(128)}, s32[]{:T(128)}) while((s32[]{:T(128)}, f32[4096,512]{1,0:T(8,128)}, f32[4,4096,64]{2,1,0:T(8,128)}, f32[4,64,64]{2,1,0:T(8,128)S(1)}, s32[]{:T(128)}, ...), condition=%wide.region_3.3_spmd, body=%wide.region_1.2_spmd.sunk | while | flops 3248521216 | bytes 30703800 | solution.py:34
  2466.3 46.7 all-gather.5.cloned.1.call-done
  2513.0 152.2 %while.45 = (s32[]{:T(128)}, f32[4096,512]{1,0:T(8,128)}, f32[4,4096,64]{2,1,0:T(8,128)}, f32[4,64,64]{2,1,0:T(8,128)S(1)}, s32[]{:T(128)}, /*index=5*/s32[]{:T(128)}, s32[]{:T(128)}, s32[]{:T(128)}) while((s32[]{:T(128)}, f32[4096,512]{1,0:T(8,128)}, f32[4,4096,64]{2,1,0:T(8,128)}, f32[4,64,64]{2,1,0:T(8,128)S(1)}, s32[]{:T(128)}, ...), condition=%wide.region_3.3_spmd, body=%wide.region_1.2_spmd.sunk | while | flops 3248521216 | bytes 30703800 | solution.py:34
  2678.0 46.7 all-gather.5.cloned.1.call-done
  2724.7 152.2 %while.45 = (s32[]{:T(128)}, f32[4096,512]{1,0:T(8,128)}, f32[4,4096,64]{2,1,0:T(8,128)}, f32[4,64,64]{2,1,0:T(8,128)S(1)}, s32[]{:T(128)}, /*index=5*/s32[]{:T(128)}, s32[]{:T(128)}, s32[]{:T(128)}) while((s32[]{:T(128)}, f32[4096,512]{1,0:T(8,128)}, f32[4,4096,64]{2,1,0:T(8,128)}, f32[4,64,64]{2,1,0:T(8,128)S(1)}, s32[]{:T(128)}, ...), condition=%wide.region_3.3_spmd, body=%wide.region_1.2_spmd.sunk | while | flops 3248521216 | bytes 30703800 | solution.py:34
  2889.6 46.7 all-gather.5.cloned.1.call-done
  2936.3 152.2 %while.45 = (s32[]{:T(128)}, f32[4096,512]{1,0:T(8,128)}, f32[4,4096,64]{2,1,0:T(8,128)}, f32[4,64,64]{2,1,0:T(8,128)S(1)}, s32[]{:T(128)}, /*index=5*/s32[]{:T(128)}, s32[]{:T(128)}, s32[]{:T(128)}) while((s32[]{:T(128)}, f32[4096,512]{1,0:T(8,128)}, f32[4,4096,64]{2,1,0:T(8,128)}, f32[4,64,64]{2,1,0:T(8,128)S(1)}, s32[]{:T(128)}, ...), condition=%wide.region_3.3_spmd, body=%wide.region_1.2_spmd.sunk | while | flops 3248521216 | bytes 30703800 | solution.py:34
  3101.3 46.7 all-gather.5.cloned.1.call-done
  3148.0 152.2 %while.45 = (s32[]{:T(128)}, f32[4096,512]{1,0:T(8,128)}, f32[4,4096,64]{2,1,0:T(8,128)}, f32[4,64,64]{2,1,0:T(8,128)S(1)}, s32[]{:T(128)}, /*index=5*/s32[]{:T(128)}, s32[]{:T(128)}, s32[]{:T(128)}) while((s32[]{:T(128)}, f32[4096,512]{1,0:T(8,128)}, f32[4,4096,64]{2,1,0:T(8,128)}, f32[4,64,64]{2,1,0:T(8,128)S(1)}, s32[]{:T(128)}, ...), condition=%wide.region_3.3_spmd, body=%wide.region_1.2_spmd.sunk | while | flops 3248521216 | bytes 30703800 | solution.py:34
  3312.9 46.7 all-gather.5.cloned.1.call-done
  3359.6 152.2 %while.45 = (s32[]{:T(128)}, f32[4096,512]{1,0:T(8,128)}, f32[4,4096,64]{2,1,0:T(8,128)}, f32[4,64,64]{2,1,0:T(8,128)S(1)}, s32[]{:T(128)}, /*index=5*/s32[]{:T(128)}, s32[]{:T(128)}, s32[]{:T(128)}) while((s32[]{:T(128)}, f32[4096,512]{1,0:T(8,128)}, f32[4,4096,64]{2,1,0:T(8,128)}, f32[4,64,64]{2,1,0:T(8,128)S(1)}, s32[]{:T(128)}, ...), condition=%wide.region_3.3_spmd, body=%wide.region_1.2_spmd.sunk | while | flops 3248521216 | bytes 30703800 | solution.py:34
  3524.6 46.7 all-gather.5.cloned.1.call-done
  3571.3 152.2 %while.45 = (s32[]{:T(128)}, f32[4096,512]{1,0:T(8,128)}, f32[4,4096,64]{2,1,0:T(8,128)}, f32[4,64,64]{2,1,0:T(8,128)S(1)}, s32[]{:T(128)}, /*index=5*/s32[]{:T(128)}, s32[]{:T(128)}, s32[]{:T(128)}) while((s32[]{:T(128)}, f32[4096,512]{1,0:T(8,128)}, f32[4,4096,64]{2,1,0:T(8,128)}, f32[4,64,64]{2,1,0:T(8,128)S(1)}, s32[]{:T(128)}, ...), condition=%wide.region_3.3_spmd, body=%wide.region_1.2_spmd.sunk | while | flops 3248521216 | bytes 30703800 | solution.py:34
  3736.2 46.7 all-gather.5.cloned.1.call-done
  3782.9 152.2 %while.45 = (s32[]{:T(128)}, f32[4096,512]{1,0:T(8,128)}, f32[4,4096,64]{2,1,0:T(8,128)}, f32[4,64,64]{2,1,0:T(8,128)S(1)}, s32[]{:T(128)}, /*index=5*/s32[]{:T(128)}, s32[]{:T(128)}, s32[]{:T(128)}) while((s32[]{:T(128)}, f32[4096,512]{1,0:T(8,128)}, f32[4,4096,64]{2,1,0:T(8,128)}, f32[4,64,64]{2,1,0:T(8,128)S(1)}, s32[]{:T(128)}, ...), condition=%wide.region_3.3_spmd, body=%wide.region_1.2_spmd.sunk | while | flops 3248521216 | bytes 30703800 | solution.py:34
  3947.9 46.7 all-gather.5.cloned.1.call-done
  3994.6 152.2 %while.45 = (s32[]{:T(128)}, f32[4096,512]{1,0:T(8,128)}, f32[4,4096,64]{2,1,0:T(8,128)}, f32[4,64,64]{2,1,0:T(8,128)S(1)}, s32[]{:T(128)}, /*index=5*/s32[]{:T(128)}, s32[]{:T(128)}, s32[]{:T(128)}) while((s32[]{:T(128)}, f32[4096,512]{1,0:T(8,128)}, f32[4,4096,64]{2,1,0:T(8,128)}, f32[4,64,64]{2,1,0:T(8,128)S(1)}, s32[]{:T(128)}, ...), condition=%wide.region_3.3_spmd, body=%wide.region_1.2_spmd.sunk | while | flops 3248521216 | bytes 30703800 | solution.py:34
  4159.5 46.7 all-gather.5.cloned.1.call-done
  4206.2 152.2 %while.45 = (s32[]{:T(128)}, f32[4096,512]{1,0:T(8,128)}, f32[4,4096,64]{2,1,0:T(8,128)}, f32[4,64,64]{2,1,0:T(8,128)S(1)}, s32[]{:T(128)}, /*index=5*/s32[]{:T(128)}, s32[]{:T(128)}, s32[]{:T(128)}) while((s32[]{:T(128)}, f32[4096,512]{1,0:T(8,128)}, f32[4,4096,64]{2,1,0:T(8,128)}, f32[4,64,64]{2,1,0:T(8,128)S(1)}, s32[]{:T(128)}, ...), condition=%wide.region_3.3_spmd, body=%wide.region_1.2_spmd.sunk | while | flops 3248521216 | bytes 30703800 | solution.py:34
  4371.2 46.7 all-gather.5.cloned.1.call-done
  4417.9 152.2 %while.45 = (s32[]{:T(128)}, f32[4096,512]{1,0:T(8,128)}, f32[4,4096,64]{2,1,0:T(8,128)}, f32[4,64,64]{2,1,0:T(8,128)S(1)}, s32[]{:T(128)}, /*index=5*/s32[]{:T(128)}, s32[]{:T(128)}, s32[]{:T(128)}) while((s32[]{:T(128)}, f32[4096,512]{1,0:T(8,128)}, f32[4,4096,64]{2,1,0:T(8,128)}, f32[4,64,64]{2,1,0:T(8,128)S(1)}, s32[]{:T(128)}, ...), condition=%wide.region_3.3_spmd, body=%wide.region_1.2_spmd.sunk | while | flops 3248521216 | bytes 30703800 | solution.py:34
  4582.8 46.7 all-gather.5.cloned.1.call-done
  4629.5 152.2 %while.45 = (s32[]{:T(128)}, f32[4096,512]{1,0:T(8,128)}, f32[4,4096,64]{2,1,0:T(8,128)}, f32[4,64,64]{2,1,0:T(8,128)S(1)}, s32[]{:T(128)}, /*index=5*/s32[]{:T(128)}, s32[]{:T(128)}, s32[]{:T(128)}) while((s32[]{:T(128)}, f32[4096,512]{1,0:T(8,128)}, f32[4,4096,64]{2,1,0:T(8,128)}, f32[4,64,64]{2,1,0:T(8,128)S(1)}, s32[]{:T(128)}, ...), condition=%wide.region_3.3_spmd, body=%wide.region_1.2_spmd.sunk | while | flops 3248521216 | bytes 30703800 | solution.py:34
  4794.5 46.7 all-gather.5.cloned.1.call-done
  4841.2 152.2 %while.45 = (s32[]{:T(128)}, f32[4096,512]{1,0:T(8,128)}, f32[4,4096,64]{2,1,0:T(8,128)}, f32[4,64,64]{2,1,0:T(8,128)S(1)}, s32[]{:T(128)}, /*index=5*/s32[]{:T(128)}, s32[]{:T(128)}, s32[]{:T(128)}) while((s32[]{:T(128)}, f32[4096,512]{1,0:T(8,128)}, f32[4,4096,64]{2,1,0:T(8,128)}, f32[4,64,64]{2,1,0:T(8,128)S(1)}, s32[]{:T(128)}, ...), condition=%wide.region_3.3_spmd, body=%wide.region_1.2_spmd.sunk | while | flops 3248521216 | bytes 30703800 | solution.py:34
  5006.1 46.7 all-gather.5.cloned.1.call-done
  5052.8 152.2 %while.45 = (s32[]{:T(128)}, f32[4096,512]{1,0:T(8,128)}, f32[4,4096,64]{2,1,0:T(8,128)}, f32[4,64,64]{2,1,0:T(8,128)S(1)}, s32[]{:T(128)}, /*index=5*/s32[]{:T(128)}, s32[]{:T(128)}, s32[]{:T(128)}) while((s32[]{:T(128)}, f32[4096,512]{1,0:T(8,128)}, f32[4,4096,64]{2,1,0:T(8,128)}, f32[4,64,64]{2,1,0:T(8,128)S(1)}, s32[]{:T(128)}, ...), condition=%wide.region_3.3_spmd, body=%wide.region_1.2_spmd.sunk | while | flops 3248521216 | bytes 30703800 | solution.py:34
  5217.7 46.7 all-gather.5.cloned.1.call-done
  5264.5 152.2 %while.45 = (s32[]{:T(128)}, f32[4096,512]{1,0:T(8,128)}, f32[4,4096,64]{2,1,0:T(8,128)}, f32[4,64,64]{2,1,0:T(8,128)S(1)}, s32[]{:T(128)}, /*index=5*/s32[]{:T(128)}, s32[]{:T(128)}, s32[]{:T(128)}) while((s32[]{:T(128)}, f32[4096,512]{1,0:T(8,128)}, f32[4,4096,64]{2,1,0:T(8,128)}, f32[4,64,64]{2,1,0:T(8,128)S(1)}, s32[]{:T(128)}, ...), condition=%wide.region_3.3_spmd, body=%wide.region_1.2_spmd.sunk | while | flops 3248521216 | bytes 30703800 | solution.py:34
  5429.4 46.7 all-gather.5.cloned.1.call-done
  5476.1 152.2 %while.45 = (s32[]{:T(128)}, f32[4096,512]{1,0:T(8,128)}, f32[4,4096,64]{2,1,0:T(8,128)}, f32[4,64,64]{2,1,0:T(8,128)S(1)}, s32[]{:T(128)}, /*index=5*/s32[]{:T(128)}, s32[]{:T(128)}, s32[]{:T(128)}) while((s32[]{:T(128)}, f32[4096,512]{1,0:T(8,128)}, f32[4,4096,64]{2,1,0:T(8,128)}, f32[4,64,64]{2,1,0:T(8,128)S(1)}, s32[]{:T(128)}, ...), condition=%wide.region_3.3_spmd, body=%wide.region_1.2_spmd.sunk | while | flops 3248521216 | bytes 30703800 | solution.py:34
  5641.0 46.7 all-gather.5.cloned.1.call-done
  5687.7 152.2 %while.45 = (s32[]{:T(128)}, f32[4096,512]{1,0:T(8,128)}, f32[4,4096,64]{2,1,0:T(8,128)}, f32[4,64,64]{2,1,0:T(8,128)S(1)}, s32[]{:T(128)}, /*index=5*/s32[]{:T(128)}, s32[]{:T(128)}, s32[]{:T(128)}) while((s32[]{:T(128)}, f32[4096,512]{1,0:T(8,128)}, f32[4,4096,64]{2,1,0:T(8,128)}, f32[4,64,64]{2,1,0:T(8,128)S(1)}, s32[]{:T(128)}, ...), condition=%wide.region_3.3_spmd, body=%wide.region_1.2_spmd.sunk | while | flops 3248521216 | bytes 30703800 | solution.py:34
  5852.7 46.7 all-gather.5.cloned.1.call-done
  5899.4 152.2 %while.45 = (s32[]{:T(128)}, f32[4096,512]{1,0:T(8,128)}, f32[4,4096,64]{2,1,0:T(8,128)}, f32[4,64,64]{2,1,0:T(8,128)S(1)}, s32[]{:T(128)}, /*index=5*/s32[]{:T(128)}, s32[]{:T(128)}, s32[]{:T(128)}) while((s32[]{:T(128)}, f32[4096,512]{1,0:T(8,128)}, f32[4,4096,64]{2,1,0:T(8,128)}, f32[4,64,64]{2,1,0:T(8,128)S(1)}, s32[]{:T(128)}, ...), condition=%wide.region_3.3_spmd, body=%wide.region_1.2_spmd.sunk | while | flops 3248521216 | bytes 30703800 | solution.py:34
  6111.0 152.2 %while.45 = (s32[]{:T(128)}, f32[4096,512]{1,0:T(8,128)}, f32[4,4096,64]{2,1,0:T(8,128)}, f32[4,64,64]{2,1,0:T(8,128)S(1)}, s32[]{:T(128)}, /*index=5*/s32[]{:T(128)}, s32[]{:T(128)}, s32[]{:T(128)}) while((s32[]{:T(128)}, f32[4096,512]{1,0:T(8,128)}, f32[4,4096,64]{2,1,0:T(8,128)}, f32[4,64,64]{2,1,0:T(8,128)S(1)}, s32[]{:T(128)}, ...), condition=%wide.region_3.3_spmd, body=%wide.region_1.2_spmd.sunk | while | flops 3248521216 | bytes 30703800 | solution.py:34
  6322.7 152.2 %while.45 = (s32[]{:T(128)}, f32[4096,512]{1,0:T(8,128)}, f32[4,4096,64]{2,1,0:T(8,128)}, f32[4,64,64]{2,1,0:T(8,128)S(1)}, s32[]{:T(128)}, /*index=5*/s32[]{:T(128)}, s32[]{:T(128)}, s32[]{:T(128)}) while((s32[]{:T(128)}, f32[4096,512]{1,0:T(8,128)}, f32[4,4096,64]{2,1,0:T(8,128)}, f32[4,64,64]{2,1,0:T(8,128)S(1)}, s32[]{:T(128)}, ...), condition=%wide.region_3.3_spmd, body=%wide.region_1.2_spmd.sunk | while | flops 3248521216 | bytes 30703800 | solution.py:34
  6534.3 152.2 %while.45 = (s32[]{:T(128)}, f32[4096,512]{1,0:T(8,128)}, f32[4,4096,64]{2,1,0:T(8,128)}, f32[4,64,64]{2,1,0:T(8,128)S(1)}, s32[]{:T(128)}, /*index=5*/s32[]{:T(128)}, s32[]{:T(128)}, s32[]{:T(128)}) while((s32[]{:T(128)}, f32[4096,512]{1,0:T(8,128)}, f32[4,4096,64]{2,1,0:T(8,128)}, f32[4,64,64]{2,1,0:T(8,128)S(1)}, s32[]{:T(128)}, ...), condition=%wide.region_3.3_spmd, body=%wide.region_1.2_spmd.sunk | while | flops 3248521216 | bytes 30703800 | solution.py:34
  6699.3 46.7 all-gather.5.cloned.1.call-done
  6746.0 152.2 %while.45 = (s32[]{:T(128)}, f32[4096,512]{1,0:T(8,128)}, f32[4,4096,64]{2,1,0:T(8,128)}, f32[4,64,64]{2,1,0:T(8,128)S(1)}, s32[]{:T(128)}, /*index=5*/s32[]{:T(128)}, s32[]{:T(128)}, s32[]{:T(128)}) while((s32[]{:T(128)}, f32[4096,512]{1,0:T(8,128)}, f32[4,4096,64]{2,1,0:T(8,128)}, f32[4,64,64]{2,1,0:T(8,128)S(1)}, s32[]{:T(128)}, ...), condition=%wide.region_3.3_spmd, body=%wide.region_1.2_spmd.sunk | while | flops 3248521216 | bytes 30703800 | solution.py:34
  6902.1 95.2 %all_to_all.38 = f32[4096,2,256]{2,0,1:T(8,128)S(1)} all-to-all(f32[4096,2,256]{2,0,1:T(8,128)S(1)} %bitcast.40), channel_id=1, replica_groups=mesh['row'=2,'col'=4] {'row'}, dimensions={1} | all-to-all | bytes 16777216 | tf_op jit(solution)/shard_map/all_to_all | solution.py:37
  (936 shorter events, 5447.6 us)
Async XLA Ops:
  6.5 100.9 %all-to-all-start = ((f32[2,4096,256]{2,1,0:T(8,128)}), f32[2,4096,256]{2,1,0:T(8,128)}, u32[]{:S(2)}, u32[]{:S(2)}) async-start(f32[2,4096,256]{2,1,0:T(8,128)} %bitcast.42), calls=%async_computation | async-start | bytes 16777216 | tf_op jit(solution)/shard_map/all_to_all | solution.py:16
  125.3 59.6 all-gather.5.cloned.1.call-start
  337.2 59.4 all-gather.5.cloned.1.call-start
  396.6 25.1 all-reduce.2.cloned.1.call-start
  548.8 59.4 all-gather.5.cloned.1.call-start
  608.2 25.1 all-reduce.2.cloned.1.call-start
  760.5 59.4 all-gather.5.cloned.1.call-start
  819.9 25.1 all-reduce.2.cloned.1.call-start
  972.1 59.4 all-gather.5.cloned.1.call-start
  1031.5 25.1 all-reduce.2.cloned.1.call-start
  1183.8 59.4 all-gather.5.cloned.1.call-start
  1243.2 25.1 all-reduce.2.cloned.1.call-start
  1395.4 59.4 all-gather.5.cloned.1.call-start
  1454.8 25.1 all-reduce.2.cloned.1.call-start
  1607.0 59.4 all-gather.5.cloned.1.call-start
  1666.5 25.1 all-reduce.2.cloned.1.call-start
  1818.7 59.4 all-gather.5.cloned.1.call-start
  1878.1 25.1 all-reduce.2.cloned.1.call-start
  2030.3 59.4 all-gather.5.cloned.1.call-start
  2089.8 25.1 all-reduce.2.cloned.1.call-start
  2242.0 59.4 all-gather.5.cloned.1.call-start
  2301.4 25.1 all-reduce.2.cloned.1.call-start
  2453.6 59.4 all-gather.5.cloned.1.call-start
  2513.1 25.1 all-reduce.2.cloned.1.call-start
  2665.3 59.4 all-gather.5.cloned.1.call-start
  2724.7 25.1 all-reduce.2.cloned.1.call-start
  2876.9 59.4 all-gather.5.cloned.1.call-start
  2936.3 25.1 all-reduce.2.cloned.1.call-start
  3088.6 59.4 all-gather.5.cloned.1.call-start
  3148.0 25.1 all-reduce.2.cloned.1.call-start
  3300.2 59.4 all-gather.5.cloned.1.call-start
  3359.6 25.1 all-reduce.2.cloned.1.call-start
  3511.9 59.4 all-gather.5.cloned.1.call-start
  3571.3 25.1 all-reduce.2.cloned.1.call-start
  3723.5 59.4 all-gather.5.cloned.1.call-start
  3782.9 25.1 all-reduce.2.cloned.1.call-start
  3935.2 59.4 all-gather.5.cloned.1.call-start
  3994.6 25.1 all-reduce.2.cloned.1.call-start
  4146.8 59.4 all-gather.5.cloned.1.call-start
  4206.2 25.1 all-reduce.2.cloned.1.call-start
  4358.4 59.4 all-gather.5.cloned.1.call-start
  4417.9 25.1 all-reduce.2.cloned.1.call-start
  4570.1 59.4 all-gather.5.cloned.1.call-start
  4629.5 25.1 all-reduce.2.cloned.1.call-start
  4781.7 59.4 all-gather.5.cloned.1.call-start
  4841.2 25.1 all-reduce.2.cloned.1.call-start
  4993.4 59.4 all-gather.5.cloned.1.call-start
  5052.8 25.1 all-reduce.2.cloned.1.call-start
  5205.0 59.4 all-gather.5.cloned.1.call-start
  5264.5 25.1 all-reduce.2.cloned.1.call-start
  5416.7 59.4 all-gather.5.cloned.1.call-start
  5476.1 25.1 all-reduce.2.cloned.1.call-start
  5628.3 59.4 all-gather.5.cloned.1.call-start
  5687.7 25.1 all-reduce.2.cloned.1.call-start
  5840.0 59.4 all-gather.5.cloned.1.call-start
  5899.4 25.1 all-reduce.2.cloned.1.call-start
  6051.6 59.4 all-gather.5.cloned.1.call-start
  6111.0 25.1 all-reduce.2.cloned.1.call-start
  6263.3 59.4 all-gather.5.cloned.1.call-start
  6322.7 25.1 all-reduce.2.cloned.1.call-start
  6474.9 59.4 all-gather.5.cloned.1.call-start
  6534.3 25.1 all-reduce.2.cloned.1.call-start
  6686.6 59.4 all-gather.5.cloned.1.call-start
  6746.0 25.1 all-reduce.2.cloned.1.call-start
  (97 other events, 2436.1 us)
Sparse Core Ops, SparseCore 0:
  129.0 55.9 all-gather.4
  194.3 15.7 all-reduce.1
  340.8 55.7 all-gather.4
  405.9 15.7 all-reduce.1
  552.5 55.7 all-gather.4
  617.5 15.7 all-reduce.1
  764.1 55.7 all-gather.4
  829.2 15.7 all-reduce.1
  975.8 55.7 all-gather.4
  1040.8 15.7 all-reduce.1
  1187.4 55.7 all-gather.4
  1252.5 15.7 all-reduce.1
  1399.1 55.7 all-gather.4
  1464.1 15.7 all-reduce.1
  1610.7 55.7 all-gather.4
  1675.8 15.7 all-reduce.1
  1822.4 55.7 all-gather.4
  1887.4 15.7 all-reduce.1
  2034.0 55.7 all-gather.4
  2099.1 15.7 all-reduce.1
  2245.6 55.7 all-gather.4
  2310.7 15.7 all-reduce.1
  2457.3 55.7 all-gather.4
  2522.4 15.7 all-reduce.1
  2668.9 55.7 all-gather.4
  2734.0 15.7 all-reduce.1
  2880.6 55.7 all-gather.4
  2945.6 15.7 all-reduce.1
  3092.2 55.7 all-gather.4
  3157.3 15.7 all-reduce.1
  3303.9 55.7 all-gather.4
  3368.9 15.7 all-reduce.1
  3515.5 55.7 all-gather.4
  3580.6 15.7 all-reduce.1
  3727.2 55.7 all-gather.4
  3792.2 15.7 all-reduce.1
  3938.8 55.7 all-gather.4
  4003.9 15.7 all-reduce.1
  4150.5 55.7 all-gather.4
  4215.5 15.7 all-reduce.1
  4362.1 55.7 all-gather.4
  4427.2 15.7 all-reduce.1
  4573.8 55.7 all-gather.4
  4638.8 15.7 all-reduce.1
  4785.4 55.7 all-gather.4
  4850.5 15.7 all-reduce.1
  4997.1 55.7 all-gather.4
  5062.1 15.7 all-reduce.1
  5208.7 55.7 all-gather.4
  5273.8 15.7 all-reduce.1
  5420.3 55.7 all-gather.4
  5485.4 15.7 all-reduce.1
  5632.0 55.7 all-gather.4
  5697.0 15.7 all-reduce.1
  5843.6 55.7 all-gather.4
  5908.7 15.7 all-reduce.1
  6055.3 55.7 all-gather.4
  6120.3 15.7 all-reduce.1
  6266.9 55.7 all-gather.4
  6332.0 15.7 all-reduce.1
  6478.6 55.7 all-gather.4
  6543.6 15.7 all-reduce.1
  6690.2 55.7 all-gather.4
  6755.3 15.7 all-reduce.1
  (96 shorter events, 1508.3 us)
where the time goes:
time: 7010 us
  waiting for transfers between devices  3630 us (52%)
  matrix products  2830 us (40%)
  blocking collectives  364 us (5%)
  local copies, waits for them, and re-layouts  162 us (2%)
    psum x128, waiting for transfers between devices, inner_step(): w_sum = lax.psum(w_part, 'row')  2040 us
    dot_general x128, matrix products, inner_step(): jnp.dot(v_blk, y_blk, precision=FULL_PREC, preferred_element_type=jnp.flo...  1510 us
    all_gather x32, waiting for transfers between devices, outer_step(): v_all = lax.all_gather(v_own, 'col')  1490 us
    dot_general x128, matrix products, inner_step(): lax.dot_general(v_blk, x_in, CONTRACT_ROWS, precision=FULL_PREC, preferre...  1170 us
    all_gather x32, blocking collectives, outer_step(): t_all = lax.all_gather(t_own, 'col')  269 us
    dot_general x128, matrix products, inner_step(): jnp.dot(t_blk, w_sum, precision=FULL_PREC, preferred_element_type=jnp.flo...  149 us
  transfers between devices with their start and end apart: 161, of which 161 were waited for; matrix products, arithmetic and copies ran while one was open for 0% of the time, Pallas kernels for 0%

commit v1 on v0

v1 whole, which is shorter than its diff:
```python
import functools

import jax
import jax.numpy as jnp
from jax import lax
from jax.experimental import pallas as pl
from jax.experimental.pallas import tpu as pltpu
from jax.sharding import PartitionSpec as P

HI = lax.Precision.HIGHEST
F32 = jnp.float32
BF16 = jnp.bfloat16
MESH_ID = pl.DeviceIdType.MESH
NN = (((1,), (0,)), ((), ()))
NT = (((1,), (1,)), ((), ()))

LANES = 128
STRIP = 256


def split3(a):
    a1 = a.astype(BF16)
    rest = a - a1.astype(F32)
    a2 = rest.astype(BF16)
    a3 = (rest - a2.astype(F32)).astype(BF16)
    return a1, a2, a3


def dot6(a, b, dims):
    a1, a2, a3 = a
    b1, b2, b3 = b

    def one(p, q):
        return lax.dot_general(p, q, dims, preferred_element_type=F32)

    return ((((one(a3, b1) + one(a1, b3)) + one(a2, b2)) + one(a2, b1)) + one(a1, b2)) + one(a1, b1)


def exact(a, b, dims):
    return lax.dot_general(a, b, dims, precision=HI, preferred_element_type=F32)


def kernel(blocks, v_ref, t_ref, z_ref, x_out, vg, x_ref, tg, vbuf, v1s, v2s, v3s, wt, gram, gram_q,
           send_sem, recv_sem, tsend_sem, trecv_sem, load_sem, z_sem):
    y = lax.axis_index("row")
    col = lax.axis_index("col")
    xx = col // 2
    core = lax.rem(col, 2)
    q_own = col
    q_x = (1 - xx) * 2 + core
    q_c = xx * 2 + (1 - core)
    q_xc = (1 - xx) * 2 + (1 - core)
    dev_x = (y, q_x)
    dev_y = (1 - y, q_own)
    dev_c = (y, q_c)
    dev_xc = (y, q_xc)
    half_rows = blocks * STRIP

    def rcopy(s, kind, src, dst, dev):
        return lambda: pltpu.make_async_remote_copy(
            src_ref=src, dst_ref=dst, send_sem=send_sem.at[s, kind], recv_sem=recv_sem.at[s, kind],
            device_id=dev, device_id_type=MESH_ID)

    def rows(s):
        return pl.ds(s * STRIP, half_rows - s * STRIP)

    def halves(s):
        n = half_rows - s * STRIP
        return pl.ds(s * STRIP, n // 2), pl.ds(s * STRIP + n // 2, n // 2)

    def own(s):
        return v_ref.at[rows(s), pl.ds(s * LANES, LANES)]

    def stage_a(s):
        dst = vg.at[s, y, q_own, rows(s)]
        return [rcopy(s, 0, own(s), dst, dev_x), rcopy(s, 1, own(s), dst, dev_y), rcopy(s, 2, own(s), dst, dev_c)]

    def stage_t(s):
        def tcopy(k, dev):
            return lambda: pltpu.make_async_remote_copy(
                src_ref=t_ref.at[s], dst_ref=tg.at[s, q_own], send_sem=tsend_sem.at[s, k], recv_sem=trecv_sem.at[s, k],
                device_id=dev, device_id_type=MESH_ID)

        return [tcopy(k, dev) for k, dev in enumerate((dev_x, dev_c, dev_xc))]

    def stage_f(s):
        first, second = halves(s)
        from_x = vg.at[s, y, q_x]
        from_y = vg.at[s, 1 - y, q_own]
        return [rcopy(s, 3, from_x.at[first], from_x.at[first], dev_y),
                rcopy(s, 4, from_y.at[second], from_y.at[second], dev_x),
                rcopy(s, 5, from_x.at[rows(s)], from_x.at[rows(s)], dev_c),
                rcopy(s, 6, from_y.at[rows(s)], from_y.at[rows(s)], dev_c)]

    def stage_g(s):
        first, second = halves(s)
        diag = vg.at[s, 1 - y, q_x]
        return [rcopy(s, 7, diag.at[first], diag.at[first], dev_c),
                rcopy(s, 8, diag.at[second], diag.at[second], dev_c)]

    def start_a(s):
        for c in stage_a(s) + stage_t(s):
            c().start()

    def start_f(s):
        a = stage_a(s)
        a[0]().wait_recv()
        a[1]().wait_recv()
        for c in stage_f(s):
            c().start()

    def start_g(s):
        f = stage_f(s)
        f[0]().wait_recv()
        f[1]().wait_recv()
        for c in stage_g(s):
            c().start()

    def finish(s):
        a, f, g, t = stage_a(s), stage_f(s), stage_g(s), stage_t(s)
        for c in (a[2], f[2], f[3], g[0], g[1], *t):
            c().wait_recv()
        for c in (*a, *f, *g, *t):
            c().wait_send()

    z_copy = pltpu.make_async_copy(z_ref, x_ref, z_sem.at[0])
    z_copy.start()
    t_copy = pltpu.make_async_copy(t_ref, tg.at[:, q_own], z_sem.at[1])
    t_copy.start()
    start_a(blocks - 1)
    start_a(blocks - 2)
    start_f(blocks - 1)
    t_copy.wait()
    z_copy.wait()

    lane = lax.broadcasted_iota(jnp.int32, (64, LANES), 1)
    row_h = (lax.broadcasted_iota(jnp.int32, (LANES, LANES), 0) // 64) % 2
    col_h = (lax.broadcasted_iota(jnp.int32, (LANES, LANES), 1) // 64) % 2
    same_half = jnp.where(row_h == col_h, 1.0, 0.0).astype(F32)
    next_half = jnp.where(row_h < col_h, 1.0, 0.0).astype(F32)

    def block_step(i, carry):
        for k in range(blocks):
            @pl.when(i == k)
            def _():
                s = blocks - 1 - k
                if s >= 2:
                    start_a(s - 2)
                if s >= 1:
                    start_f(s - 1)
                start_g(s)
                finish(s)

        s = blocks - 1 - i
        n = i + 1
        total = 2 * n

        def place(t):
            dy = jnp.where(t >= n, 1, 0)
            rr = t - dy * n
            yy = jnp.where(dy == 0, y, 1 - y)
            row0 = pl.multiple_of((s + rr) * STRIP, STRIP)
            return dy, yy, row0

        def load(t, slot):
            dy, yy, row0 = place(t)
            r = pl.ds(row0, STRIP)

            def put(src, q, k):
                return pltpu.make_async_copy(
                    src, vbuf.at[slot, :, pl.ds(pl.multiple_of(q * LANES, LANES), LANES)], load_sem.at[slot, k])

            @pl.when(dy == 0)
            def _():
                put(v_ref.at[r, pl.ds(pl.multiple_of(s * LANES, LANES), LANES)], q_own, 0).start()

            @pl.when(dy != 0)
            def _():
                put(vg.at[s, yy, q_own, r], q_own, 0).start()

            for k, q in ((1, q_x), (2, q_c), (3, q_xc)):
                put(vg.at[s, yy, q, r], q, k).start()

        def load_wait(slot):
            for k, q in ((0, q_own), (1, q_x), (2, q_c), (3, q_xc)):
                pltpu.make_async_copy(
                    vg.at[0, 0, 0, pl.ds(0, STRIP)],
                    vbuf.at[slot, :, pl.ds(pl.multiple_of(q * LANES, LANES), LANES)], load_sem.at[slot, k]).wait()

        wt[...] = jnp.zeros_like(wt)
        gram[...] = jnp.zeros_like(gram)
        gram_q[...] = jnp.zeros_like(gram_q)
        load(0, 0)

        def pass_one(t, c):
            slot = lax.rem(t, 2)

            @pl.when(t + 1 < total)
            def _():
                load(t + 1, 1 - slot)

            load_wait(slot)
            _, yy, row0 = place(t)
            v1, v2, v3 = split3(vbuf[slot])
            keep = pl.ds(pl.multiple_of(t * STRIP, STRIP), STRIP)
            v1s[keep, :] = v1
            v2s[keep, :] = v2
            v3s[keep, :] = v3
            xs = split3(x_ref[:, pl.ds(pl.multiple_of(yy * half_rows + row0, STRIP), STRIP)])
            wt[...] += dot6(xs, (v1, v2, v3), NN)
            v1t = v1.T
            v2t = v2.T
            one = functools.partial(lax.dot_general, dimension_numbers=NN, preferred_element_type=F32)
            gram[...] += one(v2t, v2) + one(v1t, v1)
            gram_q[...] += one(v1t, v3) + one(v1t, v2)
            return c

        lax.fori_loop(0, total, pass_one, 0)

        gq = gram_q[...]
        g = gram[...] + (gq + gq.T)

        tq = []
        for q in range(4):
            tt = tg[s, q]
            tq.append(jnp.concatenate([jnp.where(lane < 64, tt, 0.0), jnp.where(lane >= 64, tt, 0.0)], axis=0))

        def gq_blk(a, b):
            return g[a * LANES:(a + 1) * LANES, b * LANES:(b + 1) * LANES]

        def merge(ta, gab, tb):
            return -exact(exact(ta, gab, NN), tb, NN)

        zero = jnp.zeros((LANES, LANES), F32)
        t01 = merge(tq[0], gq_blk(0, 1) * same_half, tq[1])
        t23 = merge(tq[2], gq_blk(2, 3) * same_half, tq[3])
        ta = jnp.concatenate([jnp.concatenate([tq[0], t01], axis=1), jnp.concatenate([zero, tq[1]], axis=1)], axis=0)
        tb = jnp.concatenate([jnp.concatenate([tq[2], t23], axis=1), jnp.concatenate([zero, tq[3]], axis=1)], axis=0)
        gab = jnp.concatenate([jnp.concatenate([gq_blk(a, b) * same_half for b in (2, 3)], axis=1) for a in (0, 1)], axis=0)
        tab = merge(ta, gab, tb)
        zero2 = jnp.zeros((2 * LANES, 2 * LANES), F32)
        tfull = jnp.concatenate([jnp.concatenate([ta, tab], axis=1), jnp.concatenate([zero2, tb], axis=1)], axis=0)
        g3 = jnp.concatenate([jnp.concatenate([gq_blk(a, b) * next_half for b in range(4)], axis=1) for a in range(4)], axis=0)

        y1t = exact(wt[...], tfull, NT)
        yt = y1t - exact(exact(y1t, g3, NT), tfull, NT)
        ys = split3(yt)

        def pass_two(t, c):
            _, yy, row0 = place(t)
            keep = pl.ds(pl.multiple_of(t * STRIP, STRIP), STRIP)
            vs = (v1s[keep, :], v2s[keep, :], v3s[keep, :])
            cols = pl.ds(pl.multiple_of(yy * half_rows + row0, STRIP), STRIP)
            x_ref[:, cols] = x_ref[:, cols] - dot6(ys, vs, NT)
            return c

        lax.fori_loop(0, total, pass_two, 0)
        return carry

    lax.fori_loop(0, blocks, block_step, 0)
    out = pltpu.make_async_copy(x_ref, x_out, z_sem.at[0])
    out.start()
    out.wait()


def solution(mesh):
    def local_apply(v_loc, t_loc, z_loc):
        n, k = z_loc.shape
        blocks = v_loc.shape[1] // LANES
        half_rows = v_loc.shape[0]
        wide = 4 * LANES
        t_pack = t_loc.reshape(blocks, 2, 64, 64).transpose(0, 2, 1, 3).reshape(blocks, 64, LANES)
        z_t = z_loc.T
        hbm = pl.BlockSpec(memory_space=pl.ANY)
        x_t, _ = pl.pallas_call(
            functools.partial(kernel, blocks),
            out_shape=(jax.ShapeDtypeStruct((k, n), F32),
                       jax.ShapeDtypeStruct((blocks, 2, 4, half_rows, LANES), F32)),
            in_specs=[hbm, pl.BlockSpec(memory_space=pltpu.VMEM), hbm],
            out_specs=(hbm, hbm),
            scratch_shapes=[
                pltpu.VMEM((k, n), F32),
                pltpu.VMEM((blocks, 4, 64, LANES), F32),
                pltpu.VMEM((2, STRIP, wide), F32),
                pltpu.VMEM((n, wide), BF16),
                pltpu.VMEM((n, wide), BF16),
                pltpu.VMEM((n, wide), BF16),
                pltpu.VMEM((k, wide), F32),
                pltpu.VMEM((wide, wide), F32),
                pltpu.VMEM((wide, wide), F32),
                pltpu.SemaphoreType.DMA((blocks, 9)),
                pltpu.SemaphoreType.DMA((blocks, 9)),
                pltpu.SemaphoreType.DMA((blocks, 3)),
                pltpu.SemaphoreType.DMA((blocks, 3)),
                pltpu.SemaphoreType.DMA((2, 4)),
                pltpu.SemaphoreType.DMA((2,)),
            ],
            compiler_params=pltpu.CompilerParams(has_side_effects=True, vmem_limit_bytes=64000 * 1024),
        )(v_loc, t_pack, z_t)
        return x_t.T

    return jax.shard_map(
        local_apply,
        mesh=mesh,
        in_specs=(P("row", "col"), P("col", None, None), P(None, ("row", "col"))),
        out_specs=P(None, ("row", "col")),
        check_vma=False,
    )
```

time: 7010 us -> 761 us (0.11)
  waiting for transfers between devices: 3630 us -> 0 us
  matrix products: 2830 us -> 0 us
  Pallas kernels: 0 us -> 739 us
  blocking collectives: 364 us -> 0 us
  local copies, waits for them, and re-layouts: 162 us -> 21.4 us
    dot_general x384 -> x0, matrix products: 2830 us -> none  [the longest x128 1510 us: inner_step(): jnp.dot(v_blk, y_blk, precision=FULL_PREC, preferred_element_type=jnp.flo...]
    psum x128 -> x0, waiting for transfers between devices: 2040 us -> none  [inner_step(): w_sum = lax.psum(w_part, 'row')]
    all_gather x32 -> x0, waiting for transfers between devices: 1490 us -> none  [outer_step(): v_all = lax.all_gather(v_own, 'col')]
    pallas_call x0 -> x1, Pallas kernels: none -> 739 us  [local_apply(): pl.pallas_call(functools.partial(kernel, blocks), out_shape=(jax.ShapeDty...]
    all_gather x32 -> x0, blocking collectives: 269 us -> none  [outer_step(): t_all = lax.all_gather(t_own, 'col')]
    dynamic_slice x64 -> x0, local copies, waits for them, and re-layouts: 137 us -> none  [the longest x32 113 us: outer_step(): lax.dynamic_slice_in_dim(v_loc, local_idx * block_w, block_w, axis=1)]
    all_to_all x1 -> x0, blocking collectives: 95.2 us -> none  [local_apply(): return lax.all_to_all(x_two, 'row', 1, 0, tiled=True)]
    all_to_all x1 -> x0, waiting for transfers between devices: 94 us -> none  [local_apply(): x_two = lax.all_to_all(z_loc, 'row', 0, 1, tiled=True)]
  transfers between devices with their start and end apart: 161 -> 0, of which waited for: 161 -> 0; matrix products, arithmetic and copies ran while one was open for 0% -> 0% of each run, Pallas kernels for 0% -> 0%
where the time goes in v1:
time: 761 us
  Pallas kernels  739 us (97%)
  local copies, waits for them, and re-layouts  21.4 us (3%)
    pallas_call x1, Pallas kernels, local_apply(): pl.pallas_call(functools.partial(kernel, blocks), out_shape=(jax.ShapeDty...  739 us

profile of v1, /device:TPU:0, one launch (start us, length us, event | category | flops | bytes accessed | tf_op | source)
XLA Modules:
  0.0 760.5 jit_solution(8698444815732941294)
XLA Ops:
  0.0 2.0 copy.8
  2.0 1.4 reshape.7.t_ref
  3.5 8.9 %copy.5 = f32[8192,256]{0,1:T(8,128)} copy(f32[8192,256]{1,0:T(8,128)} %param.5) | data formatting | bytes 16777216 | tf_op args[2]
  12.4 739.1 %shard_map.37 = (f32[256,8192]{1,0:T(8,128)}, f32[16,2,4,4096,128]{4,3,2,1,0:T(8,128)}) custom-call(f32[4096,2048]{1,0:T(8,128)} %v_ref.1, f32[16,64,128]{2,1,0:T(8,128)} %reshape.7.t_ref, f32[256,8192]{1,0:T(8,128)} %bitcast.6), custom_call_target="tpu_custom_call" | custom-call | tf_op jit(solution)/shard_map/pallas_call | solution.py:275
  751.5 9.0 %copy.6 = f32[8192,256]{1,0:T(8,128)} copy(f32[8192,256]{0,1:T(8,128)} %bitcast.7) | data formatting | bytes 16777216 | tf_op jit(solution)/shard_map/transpose | solution.py:300

commit v2 on v1

v2 whole, which is shorter than its diff:
```python
import functools

import jax
import jax.numpy as jnp
from jax import lax
from jax.experimental import pallas as pl
from jax.experimental.pallas import tpu as pltpu
from jax.sharding import PartitionSpec as P

HI = lax.Precision.HIGHEST
F32 = jnp.float32
BF16 = jnp.bfloat16
MESH_ID = pl.DeviceIdType.MESH
NN = (((1,), (0,)), ((), ()))
NT = (((1,), (1,)), ((), ()))

LANES = 128
STRIP = 256


def split3(a):
    a1 = a.astype(BF16)
    rest = a - a1.astype(F32)
    a2 = rest.astype(BF16)
    a3 = (rest - a2.astype(F32)).astype(BF16)
    return a1, a2, a3


def dot6(a, b, dims):
    a1, a2, a3 = a
    b1, b2, b3 = b

    def one(p, q):
        return lax.dot_general(p, q, dims, preferred_element_type=F32)

    return ((((one(a3, b1) + one(a1, b3)) + one(a2, b2)) + one(a2, b1)) + one(a1, b2)) + one(a1, b1)


def exact(a, b, dims):
    return lax.dot_general(a, b, dims, precision=HI, preferred_element_type=F32)


def kernel(blocks, v_ref, t_ref, z_ref, x_out, vg, x_ref, z_buf, tg, vbuf, v1s, v2s, v3s, wt, gram, gram_q, g_in,
           send_sem, recv_sem, tsend_sem, trecv_sem, gsend_sem, grecv_sem, load_sem, z_sem):
    y = lax.axis_index("row")
    col = lax.axis_index("col")
    xx = col // 2
    core = lax.rem(col, 2)
    q_own = col
    q_x = (1 - xx) * 2 + core
    q_c = xx * 2 + (1 - core)
    q_xc = (1 - xx) * 2 + (1 - core)
    dev_x = (y, q_x)
    dev_y = (1 - y, q_own)
    dev_c = (y, q_c)
    dev_xc = (y, q_xc)
    half_rows = blocks * STRIP
    units = 2 * blocks

    def span(u):
        i, h = u // 2, u % 2
        n = i + 1
        first = (n + 1) // 2
        begin, size = (0, first) if h == 0 else (first, n - first)
        return blocks - 1 - i, (blocks - 1 - i + begin) * STRIP, size * STRIP

    def live(u):
        return 0 <= u < units and span(u)[2] > 0

    def rcopy(u, kind, src, dst, dev):
        return lambda: pltpu.make_async_remote_copy(
            src_ref=src, dst_ref=dst, send_sem=send_sem.at[u, kind], recv_sem=recv_sem.at[u, kind],
            device_id=dev, device_id_type=MESH_ID)

    def stage_a(u):
        s, begin, size = span(u)
        r = pl.ds(begin, size)
        src = v_ref.at[r, pl.ds(s * LANES, LANES)]
        dst = vg.at[s, y, q_own, r]
        return [rcopy(u, 0, src, dst, dev_x), rcopy(u, 1, src, dst, dev_y), rcopy(u, 2, src, dst, dev_c)]

    def stage_t(s):
        def tcopy(k, dev):
            return lambda: pltpu.make_async_remote_copy(
                src_ref=t_ref.at[s], dst_ref=tg.at[s, q_own], send_sem=tsend_sem.at[s, k], recv_sem=trecv_sem.at[s, k],
                device_id=dev, device_id_type=MESH_ID)

        return [tcopy(k, dev) for k, dev in enumerate((dev_x, dev_c, dev_xc))]

    def stage_f(u):
        s, begin, size = span(u)
        first, second, r = pl.ds(begin, size // 2), pl.ds(begin + size // 2, size // 2), pl.ds(begin, size)
        from_x = vg.at[s, y, q_x]
        from_y = vg.at[s, 1 - y, q_own]
        return [rcopy(u, 3, from_x.at[first], from_x.at[first], dev_y),
                rcopy(u, 4, from_y.at[second], from_y.at[second], dev_x),
                rcopy(u, 5, from_x.at[r], from_x.at[r], dev_c),
                rcopy(u, 6, from_y.at[r], from_y.at[r], dev_c)]

    def stage_g(u):
        s, begin, size = span(u)
        first, second = pl.ds(begin, size // 2), pl.ds(begin + size // 2, size // 2)
        diag = vg.at[s, 1 - y, q_x]
        return [rcopy(u, 7, diag.at[first], diag.at[first], dev_c),
                rcopy(u, 8, diag.at[second], diag.at[second], dev_c)]

    def start_a(u):
        if live(u):
            if u % 2 == 0:
                for c in stage_t(span(u)[0]):
                    c().start()
            for c in stage_a(u):
                c().start()

    def start_f(u):
        if live(u):
            a = stage_a(u)
            a[0]().wait_recv()
            a[1]().wait_recv()
            for c in stage_f(u):
                c().start()

    def start_g(u):
        if live(u):
            a, f = stage_a(u), stage_f(u)
            f[0]().wait_recv()
            f[1]().wait_recv()
            g = stage_g(u)
            for c in g:
                c().start()
            if u % 2 == 0:
                for c in stage_t(span(u)[0]):
                    c().wait_recv()
            for c in (a[2], f[2], f[3], g[0], g[1]):
                c().wait_recv()

    def drain(u):
        if live(u):
            if u % 2 == 0:
                for c in stage_t(span(u)[0]):
                    c().wait_send()
            for c in (*stage_a(u), *stage_f(u), *stage_g(u)):
                c().wait_send()

    start_a(0)
    start_a(2)
    start_a(3)
    t_copy = pltpu.make_async_copy(t_ref, tg.at[:, q_own], z_sem.at[1])
    t_copy.start()
    z_copy = pltpu.make_async_copy(z_ref, z_buf, z_sem.at[0])
    z_copy.start()
    start_f(0)
    t_copy.wait()
    z_copy.wait()

    lane = lax.broadcasted_iota(jnp.int32, (64, LANES), 1)
    row_h = (lax.broadcasted_iota(jnp.int32, (LANES, LANES), 0) // 64) % 2
    col_h = (lax.broadcasted_iota(jnp.int32, (LANES, LANES), 1) // 64) % 2
    same_half = jnp.where(row_h == col_h, 1.0, 0.0).astype(F32)
    next_half = jnp.where(row_h < col_h, 1.0, 0.0).astype(F32)
    one = functools.partial(lax.dot_general, dimension_numbers=NN, preferred_element_type=F32)

    def block_step(i, carry):
        s = blocks - 1 - i
        n = i + 1
        n_first = (n + 1) // 2

        def row_of(t):
            return pl.multiple_of((s + t) * STRIP, STRIP)

        def x_cols(t):
            r = row_of(t)
            return (pl.ds(pl.multiple_of(y * half_rows + r, STRIP), STRIP),
                    pl.ds(pl.multiple_of((1 - y) * half_rows + r, STRIP), STRIP))

        def keep(t):
            return pl.ds(pl.multiple_of(t * 2 * STRIP, 2 * STRIP), 2 * STRIP)

        def put(src, slot, dy, q, k):
            return pltpu.make_async_copy(
                src, vbuf.at[slot, pl.ds(dy * STRIP, STRIP), pl.ds(pl.multiple_of(q * LANES, LANES), LANES)],
                load_sem.at[slot, dy, k])

        def load(t, slot):
            r = pl.ds(row_of(t), STRIP)
            put(v_ref.at[r, pl.ds(pl.multiple_of(s * LANES, LANES), LANES)], slot, 0, q_own, 0).start()
            for k, q in ((1, q_x), (2, q_c), (3, q_xc)):
                put(vg.at[s, y, q, r], slot, 0, q, k).start()
            for k, q in ((0, q_own), (1, q_x), (2, q_c), (3, q_xc)):
                put(vg.at[s, 1 - y, q, r], slot, 1, q, k).start()

        def load_wait(slot):
            for dy in (0, 1):
                for k, q in ((0, q_own), (1, q_x), (2, q_c), (3, q_xc)):
                    put(vg.at[0, 0, 0, pl.ds(0, STRIP)], slot, dy, q, k).wait()

        def take_in(lo, hi):
            @pl.when(lo < hi)
            def _():
                load(lo, lax.rem(lo, 2))

            def body(t, c):
                slot = lax.rem(t, 2)

                @pl.when(t + 1 < hi)
                def _():
                    load(t + 1, 1 - slot)

                load_wait(slot)
                v1, v2, v3 = split3(vbuf[slot])
                v1s[keep(t), :] = v1
                v2s[keep(t), :] = v2
                v3s[keep(t), :] = v3
                mine = pl.ds(pl.multiple_of((t * 2 + core) * STRIP, STRIP), STRIP)
                v1, v2, v3 = v1s[mine, :], v2s[mine, :], v3s[mine, :]
                v1t = v1.T
                v2t = v2.T
                gram[...] += one(v2t, v2) + one(v1t, v1)
                gram_q[...] += one(v1t, v3) + one(v1t, v2)
                return c

            lax.fori_loop(lo, hi, body, 0)

        def project(lo, hi):
            def body(t, c):
                own, other = x_cols(t)
                xs = split3(jnp.concatenate([x_ref[:, own], x_ref[:, other]], axis=1))
                wt[...] += dot6(xs, (v1s[keep(t), :], v2s[keep(t), :], v3s[keep(t), :]), NN)
                return c

            lax.fori_loop(lo, hi, body, 0)

        wt[...] = jnp.zeros_like(wt)
        gram[...] = jnp.zeros_like(gram)
        gram_q[...] = jnp.zeros_like(gram_q)
        own, other = x_cols(0)
        x_ref[:, own] = z_buf[own, :].T
        x_ref[:, other] = z_buf[other, :].T

        for k in range(blocks):
            @pl.when(i == k)
            def _():
                start_g(2 * k)

        take_in(0, n_first)
        project(0, n_first)

        for k in range(blocks):
            @pl.when(i == k)
            def _():
                start_g(2 * k + 1)
                start_f(2 * k + 2)
                start_a(2 * k + 4)

        take_in(n_first, n)
        gq = gram_q[...]
        gram[...] += gq + gq.T
        slot = lax.rem(i, 2)
        g_copy = pltpu.make_async_remote_copy(
            src_ref=gram, dst_ref=g_in.at[slot], send_sem=gsend_sem.at[slot], recv_sem=grecv_sem.at[slot],
            device_id=dev_c, device_id_type=MESH_ID)
        g_copy.start()
        project(n_first, n)
        g_copy.wait()
        g = gram[...] + g_in[slot]

        tq = []
        for q in range(4):
            tt = tg[s, q]
            tq.append(jnp.concatenate([jnp.where(lane < 64, tt, 0.0), jnp.where(lane >= 64, tt, 0.0)], axis=0))

        def gq_blk(a, b):
            return g[a * LANES:(a + 1) * LANES, b * LANES:(b + 1) * LANES]

        def merge(ta, gab, tb):
            return -exact(exact(ta, gab, NN), tb, NN)

        zero = jnp.zeros((LANES, LANES), F32)
        t01 = merge(tq[0], gq_blk(0, 1) * same_half, tq[1])
        t23 = merge(tq[2], gq_blk(2, 3) * same_half, tq[3])
        ta = jnp.concatenate([jnp.concatenate([tq[0], t01], axis=1), jnp.concatenate([zero, tq[1]], axis=1)], axis=0)
        tb = jnp.concatenate([jnp.concatenate([tq[2], t23], axis=1), jnp.concatenate([zero, tq[3]], axis=1)], axis=0)
        gab = jnp.concatenate([jnp.concatenate([gq_blk(a, b) * same_half for b in (2, 3)], axis=1) for a in (0, 1)], axis=0)
        tab = merge(ta, gab, tb)
        zero2 = jnp.zeros((2 * LANES, 2 * LANES), F32)
        tfull = jnp.concatenate([jnp.concatenate([ta, tab], axis=1), jnp.concatenate([zero2, tb], axis=1)], axis=0)
        g3 = jnp.concatenate([jnp.concatenate([gq_blk(a, b) * next_half for b in range(4)], axis=1) for a in range(4)], axis=0)

        y1t = exact(wt[...], tfull, NT)
        yt = y1t - exact(exact(y1t, g3, NT), tfull, NT)
        ys = split3(yt)

        for k in range(blocks):
            @pl.when(i == k)
            def _():
                start_f(2 * k + 3)
                start_a(2 * k + 5)

        def pass_two(t, c):
            own, other = x_cols(t)
            u = dot6(ys, (v1s[keep(t), :], v2s[keep(t), :], v3s[keep(t), :]), NT)
            x_ref[:, own] = x_ref[:, own] - u[:, :STRIP]
            x_ref[:, other] = x_ref[:, other] - u[:, STRIP:]
            return c

        lax.fori_loop(0, n, pass_two, 0)
        return carry

    lax.fori_loop(0, blocks, block_step, 0)
    out = pltpu.make_async_copy(x_ref, x_out, z_sem.at[0])
    out.start()
    for u in range(units):
        drain(u)
    out.wait()


def solution(mesh):
    def local_apply(v_loc, t_loc, z_loc):
        n, k = z_loc.shape
        blocks = v_loc.shape[1] // LANES
        half_rows = v_loc.shape[0]
        wide = 4 * LANES
        t_pack = t_loc.reshape(blocks, 2, 64, 64).transpose(0, 2, 1, 3).reshape(blocks, 64, LANES)
        hbm = pl.BlockSpec(memory_space=pl.ANY)
        x_t, _ = pl.pallas_call(
            functools.partial(kernel, blocks),
            out_shape=(jax.ShapeDtypeStruct((k, n), F32),
                       jax.ShapeDtypeStruct((blocks, 2, 4, half_rows, LANES), F32)),
            in_specs=[hbm, pl.BlockSpec(memory_space=pltpu.VMEM), hbm],
            out_specs=(hbm, hbm),
            scratch_shapes=[
                pltpu.VMEM((k, n), F32),
                pltpu.VMEM((n, k), F32),
                pltpu.VMEM((blocks, 4, 64, LANES), F32),
                pltpu.VMEM((2, 2 * STRIP, wide), F32),
                pltpu.VMEM((n, wide), BF16),
                pltpu.VMEM((n, wide), BF16),
                pltpu.VMEM((n, wide), BF16),
                pltpu.VMEM((k, wide), F32),
                pltpu.VMEM((wide, wide), F32),
                pltpu.VMEM((wide, wide), F32),
                pltpu.VMEM((2, wide, wide), F32),
                pltpu.SemaphoreType.DMA((2 * blocks, 9)),
                pltpu.SemaphoreType.DMA((2 * blocks, 9)),
                pltpu.SemaphoreType.DMA((blocks, 3)),
                pltpu.SemaphoreType.DMA((blocks, 3)),
                pltpu.SemaphoreType.DMA((2,)),
                pltpu.SemaphoreType.DMA((2,)),
                pltpu.SemaphoreType.DMA((2, 2, 4)),
                pltpu.SemaphoreType.DMA((2,)),
            ],
            compiler_params=pltpu.CompilerParams(has_side_effects=True, vmem_limit_bytes=64000 * 1024),
        )(v_loc, t_pack, z_loc)
        return x_t.T

    return jax.shard_map(
        local_apply,
        mesh=mesh,
        in_specs=(P("row", "col"), P("col", None, None), P(None, ("row", "col"))),
        out_specs=P(None, ("row", "col")),
        check_vma=False,
    )
```

time: 761 us -> 697 us (0.916)
  Pallas kernels: 739 us -> 682 us
  local copies, waits for them, and re-layouts: 21.4 us -> 12.4 us
    pallas_call x1, Pallas kernels: 739 us -> 682 us  [local_apply(): pl.pallas_call(functools.partial(kernel, blocks), out_shape=(jax.ShapeDty...]
    unnamed x1 -> x0, local copies, waits for them, and re-layouts: 8.89 us -> none
where the time goes in v2:
time: 697 us; the launch traced here: 694 us
  Pallas kernels  682 us (98%)
  local copies, waits for them, and re-layouts  12.4 us (2%)
    pallas_call x1, Pallas kernels, local_apply(): pl.pallas_call(functools.partial(kernel, blocks), out_shape=(jax.ShapeDty...  682 us

profile of v2, /device:TPU:0, one launch (start us, length us, event | category | flops | bytes accessed | tf_op | source)
XLA Modules:
  0.0 694.2 jit_solution(15766194421155723791)
XLA Ops:
  0.0 2.0 copy.7
  2.0 1.4 reshape.7.t_ref
  3.4 681.7 %shard_map.37 = (f32[256,8192]{1,0:T(8,128)}, f32[16,2,4,4096,128]{4,3,2,1,0:T(8,128)}) custom-call(f32[4096,2048]{1,0:T(8,128)} %v_ref.1, f32[16,64,128]{2,1,0:T(8,128)} %reshape.7.t_ref, f32[8192,256]{1,0:T(8,128)} %z_ref.1), custom_call_target="tpu_custom_call" | custom-call | tf_op jit(solution)/shard_map/pallas_call | solution.py:325
  685.2 9.0 %copy.5 = f32[8192,256]{1,0:T(8,128)} copy(f32[8192,256]{0,1:T(8,128)} %bitcast.5) | data formatting | bytes 16777216 | tf_op jit(solution)/shard_map/transpose | solution.py:354

commit v3 on v2

--- a/solution.py
+++ b/solution.py
@@ -16,6 +16,7 @@
 
 LANES = 128
 STRIP = 256
+AHEAD = 0
 
 
 def split3(a):
@@ -27,20 +28,18 @@
 
 
 def dot6(a, b, dims):
-    a1, a2, a3 = a
-    b1, b2, b3 = b
-
-    def one(p, q):
-        return lax.dot_general(p, q, dims, preferred_element_type=F32)
-
-    return ((((one(a3, b1) + one(a1, b3)) + one(a2, b2)) + one(a2, b1)) + one(a1, b2)) + one(a1, b1)
+    (a1, a2, a3), (b1, b2, b3) = a, b
+    (over_a,), (over_b,) = dims[0]
+    lhs = jnp.concatenate([a3, a1, a2, a2, a1, a1], axis=over_a)
+    rhs = jnp.concatenate([b1, b3, b2, b1, b2, b1], axis=over_b)
+    return lax.dot_general(lhs, rhs, dims, preferred_element_type=F32)
 
 
 def exact(a, b, dims):
     return lax.dot_general(a, b, dims, precision=HI, preferred_element_type=F32)
 
 
-def kernel(blocks, v_ref, t_ref, z_ref, x_out, vg, x_ref, z_buf, tg, vbuf, v1s, v2s, v3s, wt, gram, gram_q, g_in,
+def kernel(blocks, v_ref, t_ref, z_ref, x_out, vg, x_ref, tg, vbuf, v1s, v2s, v3s, wt, gram, gram_q, g_in,
            send_sem, recv_sem, tsend_sem, trecv_sem, gsend_sem, grecv_sem, load_sem, z_sem):
     y = lax.axis_index("row")
     col = lax.axis_index("col")
@@ -53,7 +52,6 @@
     dev_x = (y, q_x)
     dev_y = (1 - y, q_own)
     dev_c = (y, q_c)
-    dev_xc = (y, q_xc)
     half_rows = blocks * STRIP
     units = 2 * blocks
 
@@ -67,6 +65,20 @@
     def live(u):
         return 0 <= u < units and span(u)[2] > 0
 
+    def relay_parts(u):
+        _, begin, size = span(u)
+        cut = size // 2 + (32 if u % 2 == 0 else 0)
+        return pl.ds(begin, cut), pl.ds(begin + cut, size - cut)
+
+    order = [u for u in range(units) if span(u)[2] > 0]
+
+    def ahead(p):
+        w, strips = p + 1, 0
+        while w < len(order) and (w < p + 3 or strips < AHEAD):
+            strips += span(order[w])[2] // STRIP
+            w += 1
+        return w
+
     def rcopy(u, kind, src, dst, dev):
         return lambda: pltpu.make_async_remote_copy(
             src_ref=src, dst_ref=dst, send_sem=send_sem.at[u, kind], recv_sem=recv_sem.at[u, kind],
@@ -80,16 +92,18 @@
         return [rcopy(u, 0, src, dst, dev_x), rcopy(u, 1, src, dst, dev_y), rcopy(u, 2, src, dst, dev_c)]
 
     def stage_t(s):
-        def tcopy(k, dev):
+        def tcopy(k, src, q, dev):
             return lambda: pltpu.make_async_remote_copy(
-                src_ref=t_ref.at[s], dst_ref=tg.at[s, q_own], send_sem=tsend_sem.at[s, k], recv_sem=trecv_sem.at[s, k],
+                src_ref=src, dst_ref=tg.at[s, q], send_sem=tsend_sem.at[s, k], recv_sem=trecv_sem.at[s, k],
                 device_id=dev, device_id_type=MESH_ID)
 
-        return [tcopy(k, dev) for k, dev in enumerate((dev_x, dev_c, dev_xc))]
+        return [tcopy(0, t_ref.at[s], q_own, dev_x), tcopy(1, t_ref.at[s], q_own, dev_c),
+                tcopy(2, tg.at[s, q_x], q_x, dev_c)]
 
     def stage_f(u):
         s, begin, size = span(u)
-        first, second, r = pl.ds(begin, size // 2), pl.ds(begin + size // 2, size // 2), pl.ds(begin, size)
+        first, second = relay_parts(u)
+        r = pl.ds(begin, size)
         from_x = vg.at[s, y, q_x]
         from_y = vg.at[s, 1 - y, q_own]
         return [rcopy(u, 3, from_x.at[first], from_x.at[first], dev_y),
@@ -98,8 +112,8 @@
                 rcopy(u, 6, from_y.at[r], from_y.at[r], dev_c)]
 
     def stage_g(u):
-        s, begin, size = span(u)
-        first, second = pl.ds(begin, size // 2), pl.ds(begin + size // 2, size // 2)
+        s = span(u)[0]
+        first, second = relay_parts(u)
         diag = vg.at[s, 1 - y, q_x]
         return [rcopy(u, 7, diag.at[first], diag.at[first], dev_c),
                 rcopy(u, 8, diag.at[second], diag.at[second], dev_c)]
@@ -107,7 +121,7 @@
     def start_a(u):
         if live(u):
             if u % 2 == 0:
-                for c in stage_t(span(u)[0]):
+                for c in stage_t(span(u)[0])[:2]:
                     c().start()
             for c in stage_a(u):
                 c().start()
@@ -119,6 +133,17 @@
             a[1]().wait_recv()
             for c in stage_f(u):
                 c().start()
+            if u % 2 == 0:
+                t = stage_t(span(u)[0])
+                t[0]().wait_recv()
+                t[2]().start()
+
+    def relay(u):
+        if live(u):
+            start_f(u)
+            p = order.index(u)
+            for w in range(ahead(p - 1), ahead(p)):
+                start_a(order[w])
 
     def start_g(u):
         if live(u):
@@ -129,7 +154,7 @@
             for c in g:
                 c().start()
             if u % 2 == 0:
-                for c in stage_t(span(u)[0]):
+                for c in stage_t(span(u)[0])[1:]:
                     c().wait_recv()
             for c in (a[2], f[2], f[3], g[0], g[1]):
                 c().wait_recv()
@@ -142,14 +167,13 @@
             for c in (*stage_a(u), *stage_f(u), *stage_g(u)):
                 c().wait_send()
 
-    start_a(0)
-    start_a(2)
-    start_a(3)
+    for w in range(ahead(-1)):
+        start_a(order[w])
     t_copy = pltpu.make_async_copy(t_ref, tg.at[:, q_own], z_sem.at[1])
     t_copy.start()
-    z_copy = pltpu.make_async_copy(z_ref, z_buf, z_sem.at[0])
+    z_copy = pltpu.make_async_copy(z_ref, x_ref, z_sem.at[0])
     z_copy.start()
-    start_f(0)
+    relay(0)
     t_copy.wait()
     z_copy.wait()
 
@@ -168,7 +192,7 @@
         def row_of(t):
             return pl.multiple_of((s + t) * STRIP, STRIP)
 
-        def x_cols(t):
+        def x_rows(t):
             r = row_of(t)
             return (pl.ds(pl.multiple_of(y * half_rows + r, STRIP), STRIP),
                     pl.ds(pl.multiple_of((1 - y) * half_rows + r, STRIP), STRIP))
@@ -215,16 +239,16 @@
                 v1, v2, v3 = v1s[mine, :], v2s[mine, :], v3s[mine, :]
                 v1t = v1.T
                 v2t = v2.T
-                gram[...] += one(v2t, v2) + one(v1t, v1)
-                gram_q[...] += one(v1t, v3) + one(v1t, v2)
+                gram[...] += one(jnp.concatenate([v2t, v1t], axis=1), jnp.concatenate([v2, v1], axis=0))
+                gram_q[...] += one(jnp.concatenate([v1t, v1t], axis=1), jnp.concatenate([v3, v2], axis=0))
                 return c
 
             lax.fori_loop(lo, hi, body, 0)
 
         def project(lo, hi):
             def body(t, c):
-                own, other = x_cols(t)
-                xs = split3(jnp.concatenate([x_ref[:, own], x_ref[:, other]], axis=1))
+                own, other = x_rows(t)
+                xs = split3(jnp.concatenate([x_ref[own, :].T, x_ref[other, :].T], axis=1))
                 wt[...] += dot6(xs, (v1s[keep(t), :], v2s[keep(t), :], v3s[keep(t), :]), NN)
                 return c
 
@@ -233,9 +257,6 @@
         wt[...] = jnp.zeros_like(wt)
         gram[...] = jnp.zeros_like(gram)
         gram_q[...] = jnp.zeros_like(gram_q)
-        own, other = x_cols(0)
-        x_ref[:, own] = z_buf[own, :].T
-        x_ref[:, other] = z_buf[other, :].T
 
         for k in range(blocks):
             @pl.when(i == k)
@@ -249,8 +270,7 @@
             @pl.when(i == k)
             def _():
                 start_g(2 * k + 1)
-                start_f(2 * k + 2)
-                start_a(2 * k + 4)
+                relay(2 * k + 2)
 
         take_in(n_first, n)
         gq = gram_q[...]
@@ -288,19 +308,18 @@
 
         y1t = exact(wt[...], tfull, NT)
         yt = y1t - exact(exact(y1t, g3, NT), tfull, NT)
-        ys = split3(yt)
+        ys = split3(yt.T)
 
         for k in range(blocks):
             @pl.when(i == k)
             def _():
-                start_f(2 * k + 3)
-                start_a(2 * k + 5)
+                relay(2 * k + 3)
 
         def pass_two(t, c):
-            own, other = x_cols(t)
-            u = dot6(ys, (v1s[keep(t), :], v2s[keep(t), :], v3s[keep(t), :]), NT)
-            x_ref[:, own] = x_ref[:, own] - u[:, :STRIP]
-            x_ref[:, other] = x_ref[:, other] - u[:, STRIP:]
+            own, other = x_rows(t)
+            u = dot6((v1s[keep(t), :], v2s[keep(t), :], v3s[keep(t), :]), ys, NN)
+            x_ref[own, :] = x_ref[own, :] - u[:STRIP]
+            x_ref[other, :] = x_ref[other, :] - u[STRIP:]
             return c
 
         lax.fori_loop(0, n, pass_two, 0)
@@ -322,14 +341,13 @@
         wide = 4 * LANES
         t_pack = t_loc.reshape(blocks, 2, 64, 64).transpose(0, 2, 1, 3).reshape(blocks, 64, LANES)
         hbm = pl.BlockSpec(memory_space=pl.ANY)
-        x_t, _ = pl.pallas_call(
+        x_new, _ = pl.pallas_call(
             functools.partial(kernel, blocks),
-            out_shape=(jax.ShapeDtypeStruct((k, n), F32),
+            out_shape=(jax.ShapeDtypeStruct((n, k), F32),
                        jax.ShapeDtypeStruct((blocks, 2, 4, half_rows, LANES), F32)),
             in_specs=[hbm, pl.BlockSpec(memory_space=pltpu.VMEM), hbm],
             out_specs=(hbm, hbm),
             scratch_shapes=[
-                pltpu.VMEM((k, n), F32),
                 pltpu.VMEM((n, k), F32),
                 pltpu.VMEM((blocks, 4, 64, LANES), F32),
                 pltpu.VMEM((2, 2 * STRIP, wide), F32),
@@ -351,7 +369,7 @@
             ],
             compiler_params=pltpu.CompilerParams(has_side_effects=True, vmem_limit_bytes=64000 * 1024),
         )(v_loc, t_pack, z_loc)
-        return x_t.T
+        return x_new
 
     return jax.shard_map(
         local_apply,

time: 697 us -> 680 us (0.976)
  Pallas kernels: 682 us -> 666 us
    pallas_call x1, Pallas kernels: 682 us -> 666 us  [local_apply(): pl.pallas_call(functools.partial(kernel, blocks), out_shape=(jax.ShapeDty...]
    transpose x1 -> x0, local copies, waits for them, and re-layouts: 9 us -> none  [local_apply(): return x_t.T]
    unnamed x0 -> x1, local copies, waits for them, and re-layouts: none -> 7.32 us
where the time goes in v3:
time: 680 us; the launch traced here: 677 us
  Pallas kernels  666 us (98%)
  local copies, waits for them, and re-layouts  10.7 us (2%)
    pallas_call x1, Pallas kernels, local_apply(): pl.pallas_call(functools.partial(kernel, blocks), out_shape=(jax.ShapeDty...  666 us

profile of v3, /device:TPU:0, one launch (start us, length us, event | category | flops | bytes accessed | tf_op | source)
XLA Modules:
  0.0 677.1 jit_solution(15583155529706712459)
XLA Ops:
  0.0 2.0 copy.6
  2.0 1.4 reshape.7.t_ref
  3.4 666.3 %shard_map.37 = (f32[8192,256]{1,0:T(8,128)}, f32[16,2,4,4096,128]{4,3,2,1,0:T(8,128)}) custom-call(f32[4096,2048]{1,0:T(8,128)} %v_ref.1, f32[16,64,128]{2,1,0:T(8,128)} %reshape.7.t_ref, f32[8192,256]{1,0:T(8,128)} %z_ref.1), custom_call_target="tpu_custom_call" | custom-call | tf_op jit(solution)/shard_map/pallas_call | solution.py:344
  669.8 7.3 %copy.8 = f32[8192,256]{1,0:T(8,128)} copy(f32[8192,256]{1,0:T(8,128)} %get-tuple-element.6) | data formatting | bytes 16777216
